TPU v7x, 256 devices: a whole 4x4x8 slice. The times are simulated.
256 devices in a mesh: sec: 16 (over z_hi, x, core), gy: 4 (over z_lo), gz: 4 (over y).
Axes of the slice: x: 4, y: 4, z: 8 (z_hi: 2, z_lo: 4; z = z_hi * 4 + z_lo), core: 2. Of those that a mesh axis runs over, the one named last changes fastest.
Arguments:
- inflow: float32 [5, 128, 1024], P(None, 'gy', 'gz'), may hold values from -6 to 6
- initial: float32 [16, 5, 128, 1024], P('sec', None, 'gy', 'gz'), may hold values from -6 to 6
- solid: int32 [16, 128, 1024], P('sec', 'gy', 'gz'), may hold values 0 or 1
- speed_y: float32 [5], replicated, may hold values from -1 to 1
- speed_z: float32 [5], replicated, may hold values from -1 to 1
- vigneron: float32 [5], replicated, may hold values from 0.2 to 0.9
- coupling: float32 [5, 5], replicated, may hold values from -2.5 to 2.5
Outputs:
- marched: float32 [16, 5, 128, 1024], P('sec', None, 'gy', 'gz')
Inputs may be any that keep to these rules, and one draw needn't show every extreme that they name: `solid`: 1 marks a cell inside the body, 0 a fluid cell.
All inputs are finite; a program needn't handle non-finite values. No bound on the sum of `solid` on one device may be relied on, other than what follows from the above.
Results may differ from a plain program's by a relative error of at most 0.00025.
Values sent between devices are 32-bit elements; how exact they have to be, the bound alone decides.
A program may use at most 64 MiB of HBM per device.

v0:
```python
import jax
import jax.numpy as jnp
from jax import lax
from jax.sharding import PartitionSpec as P

ITERS = 4
CORRECTORS = 3
NEWTON = 2


STEP_RATIO = 0.25
WENO_EPS = 1e-06


def passed_along(value, axis, steps):
    count = lax.axis_size(axis)
    initial, last = (max(0, -steps), min(count, count - steps))
    return lax.ppermute(value, axis, [(source, source + steps) for source in range(initial, last)])


def extended(block, sides, width):
    for axis, dim in sides:
        count = lax.axis_size(axis)
        forward = [(i, i + 1) for i in range(count - 1)]
        backward = [(target, source) for source, target in forward]
        low = lax.ppermute(
            lax.slice_in_dim(block, block.shape[dim] - width, None, axis=dim), axis, forward
        )
        high = lax.ppermute(lax.slice_in_dim(block, 0, width, axis=dim), axis, backward)
        block = jnp.concatenate([low, block, high], axis=dim)
    return block


def weno_face(left_far, left_near, center, right_near, right_far):
    smooth_left = (
        13.0 / 12.0 * (left_far - 2.0 * left_near + center) ** 2
        + 0.25 * (left_far - 4.0 * left_near + 3.0 * center) ** 2
    )
    smooth_middle = (
        13.0 / 12.0 * (left_near - 2.0 * center + right_near) ** 2
        + 0.25 * (left_near - right_near) ** 2
    )
    smooth_right = (
        13.0 / 12.0 * (center - 2.0 * right_near + right_far) ** 2
        + 0.25 * (3.0 * center - 4.0 * right_near + right_far) ** 2
    )
    weight_left = 0.1 / (WENO_EPS + smooth_left) ** 2
    weight_middle = 0.6 / (WENO_EPS + smooth_middle) ** 2
    weight_right = 0.3 / (WENO_EPS + smooth_right) ** 2
    guess_left = (2.0 * left_far - 7.0 * left_near + 11.0 * center) / 6.0
    guess_middle = (-left_near + 5.0 * center + 2.0 * right_near) / 6.0
    guess_right = (2.0 * center + 5.0 * right_near - right_far) / 6.0
    total = weight_left * guess_left + weight_middle * guess_middle + weight_right * guess_right
    return total / (weight_left + weight_middle + weight_right)


def sweep(padded, speeds, axis):
    count = padded.shape[axis] - 6
    plus_flux = jnp.maximum(speeds, 0.0)[:, None, None] * padded
    minus_flux = jnp.minimum(speeds, 0.0)[:, None, None] * padded

    def window(source, offset):
        return lax.slice_in_dim(source, offset, offset + count + 1, axis=axis)

    faces = weno_face(
        window(plus_flux, 0),
        window(plus_flux, 1),
        window(plus_flux, 2),
        window(plus_flux, 3),
        window(plus_flux, 4),
    )
    faces = faces + weno_face(
        window(minus_flux, 5),
        window(minus_flux, 4),
        window(minus_flux, 3),
        window(minus_flux, 2),
        window(minus_flux, 1),
    )
    return lax.slice_in_dim(faces, 1, count + 1, axis=axis) - lax.slice_in_dim(
        faces, 0, count, axis=axis
    )


def crossflow(padded, speed_y, speed_z):
    rows_part = sweep(padded[:, :, 3:-3], speed_y, 1)
    cols_part = sweep(padded[:, 3:-3, :], speed_z, 2)
    return rows_part + cols_part


def streamwise(field, factor):
    return field + factor * field**3 / (1.0 + field**2)


def slope(field, factor):
    return 1.0 + factor * field**2 * (3.0 + field**2) / (1.0 + field**2) ** 2


def correct(padded, current, upstream, diff, blocked, params):
    speed_y, speed_z, vigneron, coupling = params
    factor = vigneron[:, None, None]
    mixed = jnp.einsum("vw,wyz->vyz", coupling, current, precision=lax.Precision.HIGHEST)
    target = (
        streamwise(upstream, factor)
        - STEP_RATIO * crossflow(padded, speed_y, speed_z)
        + STEP_RATIO * mixed
        - (1.0 - factor) * diff
    )
    guess = current
    for newton_index in range(NEWTON):
        guess = guess - (streamwise(guess, factor) - target) / slope(guess, factor)
    return jnp.where(blocked[None], 0.0, guess)


def per_device(inflow, initial, solid, speed_y, speed_z, vigneron, coupling):
    params = (speed_y, speed_z, vigneron, coupling)
    sections = lax.axis_size("sec")
    position = lax.axis_index("sec")
    is_first = position == 0
    start_plane = initial[0]
    guess_above = passed_along(start_plane, "sec", 1)
    guess_above = jnp.where(is_first, inflow, guess_above)
    solid_tile = solid[0] != 0

    def station(upstream, diff):
        current = upstream
        for corrector_index in range(CORRECTORS):
            padded = extended(current, (("gy", 1), ("gz", 2)), 3)
            current = correct(padded, current, upstream, diff, solid_tile, params)
        return current

    def advance(step_index, carry):
        sent, own_prior, upstream_prior = carry
        received = passed_along(sent, "sec", 1)
        received = jnp.where(is_first, inflow, received)
        iterate = step_index - position + 1
        active = (iterate >= 1) & (iterate <= ITERS)
        updated = station(received, own_prior - upstream_prior)
        own_next = jnp.where(active, updated, own_prior)
        upstream_next = jnp.where(active, received, upstream_prior)
        return (own_next, own_next, upstream_next)

    result = lax.fori_loop(
        0, ITERS + sections - 1, advance, (start_plane, start_plane, guess_above)
    )
    return result[1][None]


def solution(mesh):
    return jax.shard_map(
        per_device,
        mesh=mesh,
        in_specs=(
            P(None, "gy", "gz"),
            P("sec", None, "gy", "gz"),
            P("sec", "gy", "gz"),
            P(),
            P(),
            P(),
            P(),
        ),
        out_specs=P("sec", None, "gy", "gz"),
        check_vma=False,
    )
```

profile of v0, /device:TPU:216, one launch (start us, length us, event | category | flops | bytes accessed | tf_op | source)
XLA Modules:
  0.0 1384.3 jit_solution(14604490556540504122)
XLA Ops:
  3.7 11.7 collective-permute-done.13
  15.4 1368.3 %while.17 = (s32[]{:T(128)}, f32[5,32,256]{2,1,0:T(8,128)S(1)}, f32[5,32,256]{2,1,0:T(8,128)S(1)}, f32[5,32,256]{2,1,0:T(8,128)S(1)}, s32[]{:T(128)}, /*index=5*...) while((s32[]{:T(128)}, f32[5,32,256]{2,1,0:T(8,128)S(1)}, ...), condition=%wide.region_1.2_spmd, body=%wide.region_0.1_spmd.sunk | while | flops 46623872 | bytes 23467136 | solution.py:142
  17.4 11.8 collective-permute-done
  90.9 10.9 collective-permute-done
  139.9 4.7 collective-permute-start.10
  163.1 10.7 collective-permute-done
  211.8 4.7 collective-permute-start.10
  235.0 10.7 collective-permute-done
  307.0 10.7 collective-permute-done
  378.9 10.7 collective-permute-done
  450.8 10.7 collective-permute-done
  522.7 10.8 collective-permute-done
  594.6 10.7 collective-permute-done
  666.6 10.8 collective-permute-done
  715.3 4.7 collective-permute-start.10
  738.5 10.8 collective-permute-done
  787.2 4.7 collective-permute-start.10
  810.4 10.8 collective-permute-done
  859.1 4.7 collective-permute-start.10
  882.3 10.8 collective-permute-done
  931.0 4.7 collective-permute-start.10
  954.2 10.8 collective-permute-done
  1002.9 4.7 collective-permute-start.10
  1026.1 10.7 collective-permute-done
  1074.9 4.7 collective-permute-start.10
  1098.0 10.8 collective-permute-done
  1146.8 4.7 collective-permute-start.10
  1169.9 10.8 collective-permute-done
  1218.7 4.7 collective-permute-start.10
  1241.8 10.8 collective-permute-done
  1290.6 4.7 collective-permute-start.10
  1313.7 10.7 collective-permute-done
  (1053 shorter events, 1108.2 us)
Async XLA Ops:
  0.9 14.4 %collective-permute-start.13 = (f32[5,32,256]{2,1,0:T(8,128)S(1)}, f32[5,32,256]{2,1,0:T(8,128)S(1)}, u32[]{:S(2)}, u32[]{:S(2)}) collective-permute-start(f32[5,32,256]{2,1,0:T(8,128)S(1)} %bitcast.41), channel_id=1, source_target_pairs={{0,16},{16,32},{32,48},{48,64},{64,80},{80,96},{96,112},{112,128},... | collective-permute-start | bytes 491528 | tf_op jit(solution)/shard_map/ppermute | solution.py:18
  15.4 13.7 collective-permute-start
  67.6 7.1 collective-permute-start.10
  88.9 12.9 collective-permute-start
  139.9 7.1 collective-permute-start.10
  161.1 12.7 collective-permute-start
  211.8 7.1 collective-permute-start.10
  233.0 12.7 collective-permute-start
  305.0 12.7 collective-permute-start
  355.7 7.1 collective-permute-start.10
  376.9 12.7 collective-permute-start
  427.6 7.1 collective-permute-start.10
  448.8 12.7 collective-permute-start
  499.5 7.1 collective-permute-start.10
  520.7 12.8 collective-permute-start
  592.6 12.7 collective-permute-start
  643.4 7.1 collective-permute-start.10
  664.6 12.8 collective-permute-start
  715.3 7.1 collective-permute-start.10
  736.5 12.8 collective-permute-start
  787.2 7.1 collective-permute-start.10
  808.4 12.8 collective-permute-start
  859.1 7.1 collective-permute-start.10
  880.3 12.8 collective-permute-start
  931.0 7.1 collective-permute-start.10
  952.2 12.8 collective-permute-start
  1024.1 12.7 collective-permute-start
  1096.0 12.8 collective-permute-start
  1168.0 12.8 collective-permute-start
  1239.9 12.8 collective-permute-start
  1311.8 12.7 collective-permute-start
  1362.5 7.1 collective-permute-start.10
  (223 other events, 1296.6 us)
where the time goes:
time: 1390 us; the launch traced here: 1380 us
  waiting for transfers between devices  600 us (43%)
  starting transfers between devices  576 us (41%)
  other arithmetic  168 us (12%)
  matrix products  25.1 us (2%)
    ppermute x114, waiting for transfers between devices, extended(): lax.ppermute(lax.slice_in_dim(block, block.shape[dim] - width, None, axis...  320 us
    ppermute x114, starting transfers between devices, extended(): lax.ppermute(lax.slice_in_dim(block, block.shape[dim] - width, None, axis...  282 us
    ppermute x114, starting transfers between devices, extended(): lax.ppermute(lax.slice_in_dim(block, 0, width, axis=dim), axis, backward)  256 us
    ppermute x20, waiting for transfers between devices, passed_along(): lax.ppermute(value, axis, [(source, source + steps) for source in range(i...  217 us
    add x114, other arithmetic, sweep(): faces + weno_face(window(minus_flux, 5), window(minus_flux, 4), window(mi...  129 us
    ppermute x114, waiting for transfers between devices, extended(): lax.ppermute(lax.slice_in_dim(block, 0, width, axis=dim), axis, backward)  62.7 us
    ppermute x20, starting transfers between devices, passed_along(): lax.ppermute(value, axis, [(source, source + steps) for source in range(i...  38.4 us
  transfers between devices with their start and end apart: 248, of which 134 were waited for; matrix products, arithmetic and copies ran while one was open for 6% of the time, Pallas kernels for 0%

commit v1 on v0

v1 whole, which is shorter than its diff:
```python
import jax
import jax.numpy as jnp
from jax import lax
from jax.experimental import pallas as pl
from jax.experimental.pallas import tpu as pltpu
from jax.sharding import PartitionSpec as P

ITERS = 4
CORRECTORS = 3
NEWTON = 2
NVAR = 5
STEP_RATIO = 0.25
WENO_EPS = 1e-06
ROWS = 32
LANES = 128
TOP = 8
MESH = pl.DeviceIdType.MESH


def inverse(x):
    r = pl.reciprocal(x, approx=True)
    return r * (2.0 - x * r)


def direction(speed):
    pos = speed >= 0.0

    def pick(a, b):
        return jnp.where(pos, jnp.float32(a), jnp.float32(b))

    return dict(
        s2=speed * speed,
        left=pick(1 / 6, 0.5),
        right=pick(0.5, 1 / 6),
        l1=pick(5 / 6, -4 / 6),
        l2=pick(-2 / 6, 1 / 6),
        m1=pick(1 / 6, -2 / 6),
        m2=pick(2 / 6, -1 / 6),
        r1=pick(4 / 6, -5 / 6),
        r2=pick(-1 / 6, 2 / 6),
    )


def face(a, b, c, d, e, k):
    ba, cb, dc, ed = b - a, c - b, d - c, e - d
    s2 = k["s2"]

    def weight(second, first):
        smooth = (13.0 / 3.0) * (second * second) + first * first
        r = inverse(4.0 * WENO_EPS + s2 * smooth)
        return r * r

    left2, mid2, right2 = cb - ba, dc - cb, ed - dc
    gl = k["left"] * weight(left2, left2 + 2.0 * cb)
    gm = weight(mid2, dc + cb)
    gr = k["right"] * weight(right2, right2 - 2.0 * dc)
    ql = k["l1"] * cb + k["l2"] * ba
    qm = k["m1"] * cb + k["m2"] * dc
    qr = k["r1"] * dc + k["r2"] * ed
    return c + (gl * ql + gm * qm + gr * qr) * inverse(gl + gm + gr)


def kernel(inflow, initial, solid, sy, sz, vig, coup, out,
           X, GA, BD, T0, ZS, ZR, ys_send, ys_recv, zs_send, zs_recv,
           pl_send, pl_recv, ga_send, ga_recv):
    p, y, z = lax.axis_index("sec"), lax.axis_index("gy"), lax.axis_index("gz")
    np_, ny, nz = lax.axis_size("sec"), lax.axis_size("gy"), lax.axis_size("gz")
    first, not_last = p == 0, p < np_ - 1
    sides = (
        ("y", 0, y > 0, y - 1, z), ("y", 1, y < ny - 1, y + 1, z),
        ("z", 0, z > 0, y, z - 1), ("z", 1, z < nz - 1, y, z + 1),
    )
    lane = lax.broadcasted_iota(jnp.int32, (8, LANES), 1)

    barrier = pltpu.get_barrier_semaphore()
    count = jnp.int32(0)
    for _, _, there, yy, zz in sides:
        count = count + there.astype(jnp.int32)

        @pl.when(there)
        def _():
            pl.semaphore_signal(barrier, inc=1, device_id=(p, yy, zz), device_id_type=MESH)

        @pl.when(there & (p > 0))
        def _():
            pl.semaphore_signal(barrier, inc=1, device_id=(p - 1, yy, zz), device_id_type=MESH)

    @pl.when(p > 0)
    def _():
        pl.semaphore_signal(barrier, inc=1, device_id=(p - 1, y, z), device_id_type=MESH)

    for kind, side, there, _, _ in sides:
        @pl.when(jnp.logical_not(there))
        def _():
            if kind == "y":
                at = 0 if side == 0 else TOP + ROWS
                zero = jnp.zeros((NVAR, 2, 8, LANES), jnp.float32)
                for k in range(ITERS):
                    for c in range(CORRECTORS):
                        X[k, c, :, :, at:at + 8, :] = zero
            else:
                for k in range(ITERS):
                    for c in range(CORRECTORS):
                        ZR[k, c, side] = jnp.zeros((8, LANES), jnp.float32)

    @pl.when(first)
    def _():
        for v in range(NVAR):
            for b in range(2):
                q = inflow[v, :, b * LANES:(b + 1) * LANES]
                for k in range(ITERS):
                    X[k, 0, v, b, TOP:TOP + ROWS, :] = q

    pl.semaphore_wait(barrier, count + not_last.astype(jnp.int32) * (1 + count))

    def ga_copy():
        return pltpu.make_async_remote_copy(
            src_ref=initial.at[0], dst_ref=GA, send_sem=ga_send, recv_sem=ga_recv,
            device_id=(p + 1, y, z), device_id_type=MESH)

    def plane_copy(k, v):
        return pltpu.make_async_remote_copy(
            src_ref=X.at[k, 3, v, :, TOP:TOP + ROWS, :],
            dst_ref=X.at[k, 0, v, :, TOP:TOP + ROWS, :],
            send_sem=pl_send.at[k, v], recv_sem=pl_recv.at[k, v],
            device_id=(p + 1, y, z), device_id_type=MESH)

    def side_copy(kind, side, k, source, slot, target):
        other = 1 - side
        if kind == "y":
            src = TOP if side == 0 else TOP + ROWS - 8
            dst = TOP + ROWS if side == 0 else 0
            return pltpu.make_async_remote_copy(
                src_ref=X.at[k, source, :, :, src:src + 8, :],
                dst_ref=X.at[k, slot, :, :, dst:dst + 8, :],
                send_sem=ys_send.at[k, source, side], recv_sem=ys_recv.at[k, slot, other],
                device_id=target, device_id_type=MESH)
        return pltpu.make_async_remote_copy(
            src_ref=ZS.at[k, source, side], dst_ref=ZR.at[k, slot, other],
            send_sem=zs_send.at[k, source, side], recv_sem=zs_recv.at[k, slot, other],
            device_id=target, device_id_type=MESH)

    def pack(k, source):
        low = jnp.zeros((8, LANES), jnp.float32)
        high = jnp.zeros((8, LANES), jnp.float32)
        for i in range(NVAR * 4):
            v, g = divmod(i, 4)
            rows = slice(TOP + 8 * g, TOP + 8 * g + 8)
            mine = (lane >= 4 * i) & (lane < 4 * i + 4)
            a = X[k, source, v, 0, rows, :]
            b = X[k, source, v, 1, rows, :]
            low = jnp.where(mine, pltpu.roll(a, 4 * i, 1) if i else a, low)
            high = jnp.where(mine, pltpu.roll(b, 4 * i + 4, 1), high)
        ZS[k, source, 0] = low
        ZS[k, source, 1] = high

    def send_sides(k, source, slot, section):
        for kind, side, there, yy, zz in sides:
            @pl.when(there)
            def _():
                side_copy(kind, side, k, source, slot, (section, yy, zz)).start()

    def wait_sides(k, slot):
        for kind, side, there, yy, zz in sides:
            @pl.when(there)
            def _():
                side_copy(kind, 1 - side, k, slot, slot, (p, yy, zz)).wait_recv()

    @pl.when(first)
    def _():
        for k in range(ITERS):
            pack(k, 0)
        for k in range(ITERS):
            send_sides(k, 0, 0, p)

    @pl.when(not_last)
    def _():
        ga_copy().start()

    @pl.when(first)
    def _():
        for v in range(NVAR):
            for b in range(2):
                cols = slice(b * LANES, (b + 1) * LANES)
                BD[v, b] = (1.0 - vig[v]) * (initial[0, v, :, cols] - inflow[v, :, cols])

    @pl.when(jnp.logical_not(first))
    def _():
        ga_copy().wait_recv()
        for v in range(NVAR):
            for b in range(2):
                cols = slice(b * LANES, (b + 1) * LANES)
                BD[v, b] = (1.0 - vig[v]) * (initial[0, v, :, cols] - GA[v, :, cols])

    def corrector(c, k):
        wait_sides(k, c)
        halo_left, halo_right = ZR[k, c, 0], ZR[k, c, 1]
        q = [[X[k, c, v, b, TOP:TOP + ROWS, :] for b in range(2)] for v in range(NVAR)]
        for v in range(NVAR):
            f = vig[v]
            speed = sz[v]
            const = direction(speed)
            pos = jnp.full((ROWS, LANES), speed, jnp.float32) >= 0.0
            halo = []
            for g in range(4):
                i = 4 * v + g
                r = pltpu.roll(halo_right, 128 - 4 * i, 1) if i else halo_right
                halo.append(jnp.where(lane < 64, r, pltpu.roll(halo_left, 124 - 4 * i, 1)))
            u = jnp.concatenate(q[v] + [jnp.concatenate(halo, 0)], 1)
            w = u.shape[1]
            flux = face(pltpu.roll(u, 2, 1), pltpu.roll(u, 1, 1), u,
                        pltpu.roll(u, w - 1, 1), pltpu.roll(u, w - 2, 1), const)
            before, after = pltpu.roll(flux, 1, 1), pltpu.roll(flux, w - 1, 1)
            for b in range(2):
                cols = slice(b * LANES, (b + 1) * LANES)
                div = speed * (jnp.where(pos, flux[:, cols], after[:, cols])
                               - jnp.where(pos, before[:, cols], flux[:, cols]))
                row_speed = sy[v]
                row_const = direction(row_speed)
                row_pos = jnp.full((ROWS, LANES), row_speed, jnp.float32) >= 0.0
                s = [X[k, c, v, b, TOP - 3 + o:TOP - 3 + o + ROWS + 2, :] for o in range(5)]
                rf = face(*s, row_const)
                f0, f1, f2 = rf[0:ROWS], rf[1:ROWS + 1], rf[2:ROWS + 2]
                div = div + row_speed * (jnp.where(row_pos, f1, f2) - jnp.where(row_pos, f0, f1))
                mixed = coup[v, 0] * q[0][b]
                for o in range(1, NVAR):
                    mixed = mixed + coup[v, o] * q[o][b]
                target = T0[v, b] + STEP_RATIO * (mixed - div)
                guess = q[v][b]
                for _ in range(NEWTON):
                    sq = guess * guess
                    r = inverse(1.0 + sq)
                    t = sq * r
                    value = guess + f * (guess * t)
                    slope = 1.0 + f * (t * ((3.0 + sq) * r))
                    guess = guess - (value - target) * inverse(slope)
                X[k, c + 1, v, b, TOP:TOP + ROWS, :] = jnp.where(
                    solid[0, :, cols] != 0, 0.0, guess)

            @pl.when((c == CORRECTORS - 1) & not_last)
            def _():
                plane_copy(k, v).start()

        @pl.when((c < CORRECTORS - 1) | not_last)
        def _():
            pack(k, c + 1)

        @pl.when(c < CORRECTORS - 1)
        def _():
            send_sides(k, c + 1, c + 1, p)

        @pl.when((c == CORRECTORS - 1) & not_last)
        def _():
            send_sides(k, c + 1, 0, p + 1)

        return k

    def iterate(k, carry):
        @pl.when(jnp.logical_not(first))
        def _():
            for v in range(NVAR):
                plane_copy(k, v).wait_recv()

        for v in range(NVAR):
            for b in range(2):
                up = X[k, 0, v, b, TOP:TOP + ROWS, :]
                sq = up * up
                T0[v, b] = up + vig[v] * (up * (sq * inverse(1.0 + sq))) - BD[v, b]
        lax.fori_loop(0, CORRECTORS, corrector, k)
        for v in range(NVAR):
            for b in range(2):
                BD[v, b] = (1.0 - vig[v]) * (X[k, 3, v, b, TOP:TOP + ROWS, :]
                                             - X[k, 0, v, b, TOP:TOP + ROWS, :])
        return carry

    lax.fori_loop(0, ITERS, iterate, 0)
    for v in range(NVAR):
        for b in range(2):
            out[0, v, :, b * LANES:(b + 1) * LANES] = X[ITERS - 1, 3, v, b, TOP:TOP + ROWS, :]

    @pl.when(not_last)
    def _():
        ga_copy().wait_send()

    def drain(k, carry):
        @pl.when(not_last)
        def _():
            for v in range(NVAR):
                plane_copy(k, v).wait_send()
        for kind, side, there, yy, zz in sides:
            @pl.when(there)
            def _():
                for source in (1, 2):
                    side_copy(kind, side, k, source, source, (p, yy, zz)).wait_send()

            @pl.when(there & first)
            def _():
                side_copy(kind, side, k, 0, 0, (p, yy, zz)).wait_send()

            @pl.when(there & not_last)
            def _():
                side_copy(kind, side, k, 3, 0, (p + 1, yy, zz)).wait_send()
        return carry

    lax.fori_loop(0, ITERS, drain, 0)


def per_device(inflow, initial, solid, speed_y, speed_z, vigneron, coupling):
    vmem = pl.BlockSpec(memory_space=pltpu.VMEM)
    smem = pl.BlockSpec(memory_space=pltpu.SMEM)
    plane = (NVAR, 2, ROWS, LANES)
    dma = pltpu.SemaphoreType.DMA
    return pl.pallas_call(
        kernel,
        out_shape=jax.ShapeDtypeStruct(initial.shape, jnp.float32),
        in_specs=[vmem] * 3 + [smem] * 4,
        out_specs=vmem,
        scratch_shapes=[
            pltpu.VMEM((ITERS, CORRECTORS + 1, NVAR, 2, 48, LANES), jnp.float32),
            pltpu.VMEM((NVAR, ROWS, 2 * LANES), jnp.float32),
            pltpu.VMEM(plane, jnp.float32),
            pltpu.VMEM(plane, jnp.float32),
            pltpu.VMEM((ITERS, CORRECTORS + 1, 2, 8, LANES), jnp.float32),
            pltpu.VMEM((ITERS, CORRECTORS, 2, 8, LANES), jnp.float32),
            dma((ITERS, CORRECTORS + 1, 2)),
            dma((ITERS, CORRECTORS, 2)),
            dma((ITERS, CORRECTORS + 1, 2)),
            dma((ITERS, CORRECTORS, 2)),
            dma((ITERS, NVAR)),
            dma((ITERS, NVAR)),
            dma,
            dma,
        ],
        compiler_params=pltpu.CompilerParams(collective_id=0, has_side_effects=True),
    )(inflow, initial, solid, speed_y, speed_z, vigneron, coupling)


def solution(mesh):
    return jax.shard_map(
        per_device,
        mesh=mesh,
        in_specs=(
            P(None, "gy", "gz"),
            P("sec", None, "gy", "gz"),
            P("sec", "gy", "gz"),
            P(),
            P(),
            P(),
            P(),
        ),
        out_specs=P("sec", None, "gy", "gz"),
        check_vma=False,
    )
```

time: 1390 us -> 301 us (0.22)
  the two profiles are of different devices: /device:TPU:216 before, /device:TPU:231 now
where the time goes in v1:
time: 301 us
  Pallas kernels  299 us (99%)
    pallas_call x1, Pallas kernels, per_device(): pl.pallas_call(kernel, out_shape=jax.ShapeDtypeStruct(initial.shape, jnp....  299 us

profile of v1, /device:TPU:231, one launch (start us, length us, event | category | flops | bytes accessed | tf_op | source)
XLA Modules:
  0.0 300.8 jit_solution(1539351597734070391)
XLA Ops:
  0.0 299.2 %shard_map.73 = f32[1,5,32,256]{3,2,1,0:T(8,128)} custom-call(f32[5,32,256]{2,1,0:T(8,128)} %inflow.1, f32[1,5,32,256]{3,2,1,0:T(8,128)} %initial.1, s32[1,32,256]{2,1,0:T(8,128)} %solid.1, f32[5]{0:T(128)} %sy.1, f32[5]{0:T(128)} %sz.1, f32[5]{0:T(128)} %vig.1, f32[5,5]{1,0:T(8,128)} %coup.1), custom_call_target="tpu_custom_call" | custom-call | tf_op jit(solution)/shard_map/pallas_call | solution.py:313
  299.2 1.6 copy.9

commit v2 on v1

--- a/solution.py
+++ b/solution.py
@@ -61,7 +61,7 @@
 
 
 def kernel(inflow, initial, solid, sy, sz, vig, coup, out,
-           X, GA, BD, T0, ZS, ZR, ys_send, ys_recv, zs_send, zs_recv,
+           X, GA, BD, T0, T1, FS, YS, YR, ZS, ZR, ys_send, ys_recv, zs_send, zs_recv,
            pl_send, pl_recv, ga_send, ga_recv):
     p, y, z = lax.axis_index("sec"), lax.axis_index("gy"), lax.axis_index("gz")
     np_, ny, nz = lax.axis_size("sec"), lax.axis_size("gy"), lax.axis_size("gz")
@@ -89,19 +89,24 @@
     def _():
         pl.semaphore_signal(barrier, inc=1, device_id=(p - 1, y, z), device_id_type=MESH)
 
+    zero = jnp.zeros((8, LANES), jnp.float32)
+
+    def clear(k, carry):
+        for c in range(CORRECTORS):
+            for v in range(NVAR):
+                for b in range(2):
+                    X[k, c, v, b, 0:TOP, :] = zero
+                    X[k, c, v, b, TOP + ROWS:TOP + ROWS + 8, :] = zero
+        return carry
+
+    lax.fori_loop(0, ITERS, clear, 0)
     for kind, side, there, _, _ in sides:
-        @pl.when(jnp.logical_not(there))
-        def _():
-            if kind == "y":
-                at = 0 if side == 0 else TOP + ROWS
-                zero = jnp.zeros((NVAR, 2, 8, LANES), jnp.float32)
+        if kind == "z":
+            @pl.when(jnp.logical_not(there))
+            def _():
                 for k in range(ITERS):
                     for c in range(CORRECTORS):
-                        X[k, c, :, :, at:at + 8, :] = zero
-            else:
-                for k in range(ITERS):
-                    for c in range(CORRECTORS):
-                        ZR[k, c, side] = jnp.zeros((8, LANES), jnp.float32)
+                        ZR[k, c, side] = zero
 
     @pl.when(first)
     def _():
@@ -128,11 +133,8 @@
     def side_copy(kind, side, k, source, slot, target):
         other = 1 - side
         if kind == "y":
-            src = TOP if side == 0 else TOP + ROWS - 8
-            dst = TOP + ROWS if side == 0 else 0
             return pltpu.make_async_remote_copy(
-                src_ref=X.at[k, source, :, :, src:src + 8, :],
-                dst_ref=X.at[k, slot, :, :, dst:dst + 8, :],
+                src_ref=YS.at[k, source, side], dst_ref=YR.at[k, slot, other],
                 send_sem=ys_send.at[k, source, side], recv_sem=ys_recv.at[k, slot, other],
                 device_id=target, device_id_type=MESH)
         return pltpu.make_async_remote_copy(
@@ -160,8 +162,11 @@
             def _():
                 side_copy(kind, side, k, source, slot, (section, yy, zz)).start()
 
-    def wait_sides(k, slot):
+    def wait_sides(which, k, slot):
         for kind, side, there, yy, zz in sides:
+            if kind != which:
+                continue
+
             @pl.when(there)
             def _():
                 side_copy(kind, 1 - side, k, slot, slot, (p, yy, zz)).wait_recv()
@@ -169,6 +174,12 @@
     @pl.when(first)
     def _():
         for k in range(ITERS):
+            for v in range(NVAR):
+                for b in range(2):
+                    rows = pl.ds(3 * (2 * v + b), 3)
+                    cols = slice(b * LANES, (b + 1) * LANES)
+                    YS[k, 0, 0, rows, :] = inflow[v, 0:3, cols]
+                    YS[k, 0, 1, rows, :] = inflow[v, ROWS - 3:ROWS, cols]
             pack(k, 0)
         for k in range(ITERS):
             send_sides(k, 0, 0, p)
@@ -193,49 +204,79 @@
                 BD[v, b] = (1.0 - vig[v]) * (initial[0, v, :, cols] - GA[v, :, cols])
 
     def corrector(c, k):
-        wait_sides(k, c)
+        def rows_of(v, b, at, count=8):
+            return X[k, c, v, b, TOP + at:TOP + at + count, :]
+
+        def row_face(v, b, at, const):
+            return face(*[rows_of(v, b, at + o) for o in range(-2, 3)], const)
+
+        y_const = [direction(sy[v]) for v in range(NVAR)]
+        z_const = [direction(sz[v]) for v in range(NVAR)]
+        y_pos = [jnp.full((8, LANES), sy[v], jnp.float32) >= 0.0 for v in range(NVAR)]
+
+        for v in range(NVAR):
+            for g in range(4):
+                for b in range(2):
+                    mixed = coup[v, 0] * rows_of(0, b, 8 * g)
+                    for o in range(1, NVAR):
+                        mixed = mixed + coup[v, o] * rows_of(o, b, 8 * g)
+                    rows = slice(8 * g, 8 * g + 8)
+                    T1[v, b, rows, :] = T0[v, b, rows, :] + STEP_RATIO * mixed
+            for b in range(2):
+                for g in range(4):
+                    FS[v, b, TOP + 8 * g:TOP + 8 * g + 8, :] = row_face(v, b, 8 * g, y_const[v])
+
+        wait_sides("y", k, c)
+        for kind, side, there, _, _ in sides:
+            if kind == "y":
+                @pl.when(there)
+                def _():
+                    at = TOP - 3 if side == 0 else TOP + ROWS
+                    for i in range(2 * NVAR):
+                        X[k, c, i // 2, i % 2, at:at + 3, :] = YR[k, c, side, 3 * i:3 * i + 3, :]
+        for v in range(NVAR):
+            for b in range(2):
+                for at in (-1, ROWS - 7):
+                    FS[v, b, TOP + at:TOP + at + 8, :] = row_face(v, b, at, y_const[v])
+
+        wait_sides("z", k, c)
         halo_left, halo_right = ZR[k, c, 0], ZR[k, c, 1]
-        q = [[X[k, c, v, b, TOP:TOP + ROWS, :] for b in range(2)] for v in range(NVAR)]
         for v in range(NVAR):
             f = vig[v]
-            speed = sz[v]
-            const = direction(speed)
-            pos = jnp.full((ROWS, LANES), speed, jnp.float32) >= 0.0
-            halo = []
+            pos = jnp.full((8, 2 * LANES), sz[v], jnp.float32) >= 0.0
             for g in range(4):
                 i = 4 * v + g
-                r = pltpu.roll(halo_right, 128 - 4 * i, 1) if i else halo_right
-                halo.append(jnp.where(lane < 64, r, pltpu.roll(halo_left, 124 - 4 * i, 1)))
-            u = jnp.concatenate(q[v] + [jnp.concatenate(halo, 0)], 1)
-            w = u.shape[1]
-            flux = face(pltpu.roll(u, 2, 1), pltpu.roll(u, 1, 1), u,
-                        pltpu.roll(u, w - 1, 1), pltpu.roll(u, w - 2, 1), const)
-            before, after = pltpu.roll(flux, 1, 1), pltpu.roll(flux, w - 1, 1)
-            for b in range(2):
-                cols = slice(b * LANES, (b + 1) * LANES)
-                div = speed * (jnp.where(pos, flux[:, cols], after[:, cols])
-                               - jnp.where(pos, before[:, cols], flux[:, cols]))
-                row_speed = sy[v]
-                row_const = direction(row_speed)
-                row_pos = jnp.full((ROWS, LANES), row_speed, jnp.float32) >= 0.0
-                s = [X[k, c, v, b, TOP - 3 + o:TOP - 3 + o + ROWS + 2, :] for o in range(5)]
-                rf = face(*s, row_const)
-                f0, f1, f2 = rf[0:ROWS], rf[1:ROWS + 1], rf[2:ROWS + 2]
-                div = div + row_speed * (jnp.where(row_pos, f1, f2) - jnp.where(row_pos, f0, f1))
-                mixed = coup[v, 0] * q[0][b]
-                for o in range(1, NVAR):
-                    mixed = mixed + coup[v, o] * q[o][b]
-                target = T0[v, b] + STEP_RATIO * (mixed - div)
-                guess = q[v][b]
-                for _ in range(NEWTON):
-                    sq = guess * guess
-                    r = inverse(1.0 + sq)
-                    t = sq * r
-                    value = guess + f * (guess * t)
-                    slope = 1.0 + f * (t * ((3.0 + sq) * r))
-                    guess = guess - (value - target) * inverse(slope)
-                X[k, c + 1, v, b, TOP:TOP + ROWS, :] = jnp.where(
-                    solid[0, :, cols] != 0, 0.0, guess)
+                right = pltpu.roll(halo_right, LANES - 4 * i, 1) if i else halo_right
+                halo = jnp.where(lane < 64, right, pltpu.roll(halo_left, 124 - 4 * i, 1))
+                u = jnp.concatenate([rows_of(v, 0, 8 * g), rows_of(v, 1, 8 * g), halo], 1)
+                w = u.shape[1]
+                flux = face(pltpu.roll(u, 2, 1), pltpu.roll(u, 1, 1), u,
+                            pltpu.roll(u, w - 1, 1), pltpu.roll(u, w - 2, 1), z_const[v])
+                before, after = pltpu.roll(flux, 1, 1), pltpu.roll(flux, w - 1, 1)
+                inner = slice(0, 2 * LANES)
+                div = (STEP_RATIO * sz[v]) * jnp.where(
+                    pos, (flux - before)[:, inner], (after - flux)[:, inner])
+                for b in range(2):
+                    rows = slice(8 * g, 8 * g + 8)
+                    target = T1[v, b, rows, :] - div[:, b * LANES:(b + 1) * LANES]
+                    f0, f1, f2 = [FS[v, b, TOP + 8 * g + o:TOP + 8 * g + o + 8, :] for o in (-1, 0, 1)]
+                    target = target - (STEP_RATIO * sy[v]) * jnp.where(y_pos[v], f1 - f0, f2 - f1)
+                    guess = rows_of(v, b, 8 * g)
+                    for _ in range(NEWTON):
+                        sq = guess * guess
+                        r = inverse(1.0 + sq)
+                        t = sq * r
+                        value = guess + f * (guess * t)
+                        slope = 1.0 + f * (t * ((3.0 + sq) * r))
+                        guess = guess - (value - target) * inverse(slope)
+                    guess = jnp.where(
+                        solid[0, rows, b * LANES:(b + 1) * LANES] != 0, 0.0, guess)
+                    X[k, c + 1, v, b, TOP + 8 * g:TOP + 8 * g + 8, :] = guess
+                    at = pl.ds(3 * (2 * v + b), 3)
+                    if g == 0:
+                        YS[k, c + 1, 0, at, :] = guess[0:3]
+                    if g == 3:
+                        YS[k, c + 1, 1, at, :] = guess[5:8]
 
             @pl.when((c == CORRECTORS - 1) & not_last)
             def _():
@@ -320,6 +361,10 @@
             pltpu.VMEM((NVAR, ROWS, 2 * LANES), jnp.float32),
             pltpu.VMEM(plane, jnp.float32),
             pltpu.VMEM(plane, jnp.float32),
+            pltpu.VMEM(plane, jnp.float32),
+            pltpu.VMEM((NVAR, 2, 48, LANES), jnp.float32),
+            pltpu.VMEM((ITERS, CORRECTORS + 1, 2, 32, LANES), jnp.float32),
+            pltpu.VMEM((ITERS, CORRECTORS, 2, 32, LANES), jnp.float32),
             pltpu.VMEM((ITERS, CORRECTORS + 1, 2, 8, LANES), jnp.float32),
             pltpu.VMEM((ITERS, CORRECTORS, 2, 8, LANES), jnp.float32),
             dma((ITERS, CORRECTORS + 1, 2)),

time: 301 us -> 269 us (0.89)
  Pallas kernels: 299 us -> 267 us
    pallas_call x1, Pallas kernels: 299 us -> 267 us  [per_device(): pl.pallas_call(kernel, out_shape=jax.ShapeDtypeStruct(initial.shape, jnp....]
where the time goes in v2:
time: 269 us
  Pallas kernels  267 us (99%)
    pallas_call x1, Pallas kernels, per_device(): pl.pallas_call(kernel, out_shape=jax.ShapeDtypeStruct(initial.shape, jnp....  267 us

profile of v2, /device:TPU:231, one launch (start us, length us, event | category | flops | bytes accessed | tf_op | source)
XLA Modules:
  0.0 268.6 jit_solution(6149109892775176730)
XLA Ops:
  0.0 267.0 %shard_map.73 = f32[1,5,32,256]{3,2,1,0:T(8,128)} custom-call(f32[5,32,256]{2,1,0:T(8,128)} %inflow.1, f32[1,5,32,256]{3,2,1,0:T(8,128)} %initial.1, s32[1,32,256]{2,1,0:T(8,128)} %solid.1, f32[5]{0:T(128)} %sy.1, f32[5]{0:T(128)} %sz.1, f32[5]{0:T(128)} %vig.1, f32[5,5]{1,0:T(8,128)} %coup.1), custom_call_target="tpu_custom_call" | custom-call | tf_op jit(solution)/shard_map/pallas_call | solution.py:354
  267.0 1.6 copy.9

commit v3 on v2

--- a/solution.py
+++ b/solution.py
@@ -241,6 +241,7 @@
 
         wait_sides("z", k, c)
         halo_left, halo_right = ZR[k, c, 0], ZR[k, c, 1]
+        packed = [zero, zero]
         for v in range(NVAR):
             f = vig[v]
             pos = jnp.full((8, 2 * LANES), sz[v], jnp.float32) >= 0.0
@@ -272,6 +273,9 @@
                     guess = jnp.where(
                         solid[0, rows, b * LANES:(b + 1) * LANES] != 0, 0.0, guess)
                     X[k, c + 1, v, b, TOP + 8 * g:TOP + 8 * g + 8, :] = guess
+                    mine = (lane >= 4 * i) & (lane < 4 * i + 4)
+                    by = 4 * i + 4 * b
+                    packed[b] = jnp.where(mine, pltpu.roll(guess, by, 1) if by else guess, packed[b])
                     at = pl.ds(3 * (2 * v + b), 3)
                     if g == 0:
                         YS[k, c + 1, 0, at, :] = guess[0:3]
@@ -282,9 +286,8 @@
             def _():
                 plane_copy(k, v).start()
 
-        @pl.when((c < CORRECTORS - 1) | not_last)
-        def _():
-            pack(k, c + 1)
+        for b in range(2):
+            ZS[k, c + 1, b] = packed[b]
 
         @pl.when(c < CORRECTORS - 1)
         def _():

time: 269 us -> 282 us (1.048)
  Pallas kernels: 267 us -> 281 us
    pallas_call x1, Pallas kernels: 267 us -> 281 us  [per_device(): pl.pallas_call(kernel, out_shape=jax.ShapeDtypeStruct(initial.shape, jnp....]
where the time goes in v3:
time: 282 us
  Pallas kernels  281 us (100%)
    pallas_call x1, Pallas kernels, per_device(): pl.pallas_call(kernel, out_shape=jax.ShapeDtypeStruct(initial.shape, jnp....  281 us

profile of v3, /device:TPU:231, one launch (start us, length us, event | category | flops | bytes accessed | tf_op | source)
XLA Modules:
  0.0 282.3 jit_solution(2827410788217324201)
XLA Ops:
  0.0 280.7 %shard_map.73 = f32[1,5,32,256]{3,2,1,0:T(8,128)} custom-call(f32[5,32,256]{2,1,0:T(8,128)} %inflow.1, f32[1,5,32,256]{3,2,1,0:T(8,128)} %initial.1, s32[1,32,256]{2,1,0:T(8,128)} %solid.1, f32[5]{0:T(128)} %sy.1, f32[5]{0:T(128)} %sz.1, f32[5]{0:T(128)} %vig.1, f32[5,5]{1,0:T(8,128)} %coup.1), custom_call_target="tpu_custom_call" | custom-call | tf_op jit(solution)/shard_map/pallas_call | solution.py:357
  280.7 1.6 copy.9
